TPU v7x, 256 devices: a whole 4x4x8 slice. The times are simulated.
256 devices in a mesh: grp: 4 (over y), seq: 64 (over z, x, core).
Axes of the slice: x: 4, y: 4, z: 8, core: 2. Of those that a mesh axis runs over, the one named last changes fastest.
Arguments:
- thinker_input: bfloat16 [4, 32, 3584], P(None, 'grp'), as said below
- thinker_gain: float32 [3584], replicated, may hold values from 0.25 to 1.75
- thinker_qkv: bfloat16 [3584, 4608], P('seq'), may hold values from -0.09375 to 0.09375
- thinker_out: bfloat16 [3584, 3584], P('seq'), may hold values from -0.09375 to 0.09375
- talker_proj: bfloat16 [3584, 896], P('seq'), may hold values from -0.09375 to 0.09375
- code_table: bfloat16 [8448, 896], P('seq'), may hold values from -6 to 6
- talker_gain: float32 [896], replicated, may hold values from 0.25 to 1.75
- talker_qkv: bfloat16 [896, 2560], replicated, may hold values from -0.1875 to 0.1875
- talker_out: bfloat16 [1536, 896], replicated, may hold values from -0.15625 to 0.15625
- text_keys: bfloat16 [32, 8192, 512], P('grp', 'seq'), as said below
- text_values: bfloat16 [32, 8192, 512], P('grp', 'seq'), may hold values from -72 to 72
- audio_keys: bfloat16 [32, 8192, 512], P('grp', 'seq'), as said below
- audio_values: bfloat16 [32, 8192, 512], P('grp', 'seq'), may hold values from -72 to 72
- text_len: int32 [32], P('grp'), may hold values from 2 to 8192
- audio_len: int32 [32], P('grp'), may hold values from 2 to 8192
- text_pos: int32 [32, 4], P('grp'), may hold values from 0 to 8195
- audio_pos: int32 [32, 4], P('grp'), may hold values from 0 to 8195
- code_ids: int32 [32, 4], P('grp'), may hold values from 0 to 8447
Outputs:
- thinker_hidden: bfloat16 [4, 32, 3584], P(None, 'grp')
- talker_hidden: bfloat16 [4, 32, 896], P(None, 'grp', 'seq')
Inputs may be any that keep to these rules, and one draw needn't show every extreme that they name: Cache positions 0 .. text_len - 1 of a conversation are live. Cache positions 0 .. audio_len - 1 of a conversation are live. `thinker_input`: real-valued, of order one per feature. `text_keys`: real-valued. `audio_keys`: real-valued.
All inputs are finite; a program needn't handle non-finite values.
Results may differ from a plain program's by a relative error of at most 0.028.
Values may be sent and summed in bfloat16 or wider, within the bound.
No kernel may reach another device: no remote copies, remote signals or barrier semaphores. Data moves between devices by JAX's collectives and lax.ppermute only.
A program may use at most 128 MiB of HBM per device.

v0:
```python
import functools

import jax
import jax.numpy as jnp
from jax import lax
from jax.sharding import Mesh
from jax.sharding import PartitionSpec as P

D = 3584
HQ = 28
HK = 4
HD = 128
TD = 896
AHQ = 12
AHK = 4
AHD = 128
SEQ = ("seq_0", "seq_1", "seq_2")


EPSILON = 1e-06
THETA = 1000000.0
NEGATIVE = -1e30


def all_in_one(shard, axis):
    leaves = jax.tree.leaves(shard)
    order = sorted(range(len(leaves)), key=lambda k: -leaves[k].size)
    width = (1, *leaves[order[0]].shape)[-1]
    lines = [
        jnp.pad(leaves[k].reshape(-1), (0, -leaves[k].size % width)).reshape(-1, width)
        for k in order
    ]
    both, at, found = (lax.all_gather(jnp.concatenate(lines), axis), 0, {})
    for k, line in zip(order, lines):
        section = both[:, at : at + len(line)].reshape(len(both), -1)
        found[k] = section[:, : leaves[k].size].reshape(-1, *leaves[k].shape)
        at += len(line)
    numbers = iter(range(len(leaves)))
    return jax.tree.map(lambda _: found[next(numbers)], shard)


def joined_all(shard, axes, combine):
    for axis in axes:
        pieces = all_in_one(
            jax.tree.map(
                lambda part, kind: part.astype(kind),
                shard,
                (jnp.bfloat16, jnp.bfloat16, jnp.bfloat16),
            ),
            axis,
        )
        widened = [
            jax.tree.map(lambda part, own: part[k].astype(own.dtype), pieces, shard)
            for k in range(lax.axis_size(axis))
        ]
        shard = widened[0]
        for received in widened[1:]:
            shard = combine(shard, received)
    return shard


def by_axis(shard, axes):
    return functools.reduce(lax.psum, axes, shard)


def over_pieces(shard, axis):
    return lax.all_gather(shard, axis).sum(0)


def copy_for_each(shard, axis):
    length = lax.axis_size(axis)
    return lax.all_to_all(
        jnp.broadcast_to(shard[None], (length, *shard.shape)), axis, 0, 0, tiled=True
    )


def taken_together(shard, axis):
    return copy_for_each(shard, axis).sum(axis=0)


def rotate(vectors, positions):
    width = vectors.shape[-1]
    half = width // 2
    freqs = jnp.exp(
        jnp.arange(half).astype(jnp.float32) * (-2.0 * jnp.log(jnp.float32(THETA)) / width)
    )
    angles = positions.astype(jnp.float32)[:, None] * freqs[None, :]
    cosine = jnp.cos(angles)[:, None, :]
    sine = jnp.sin(angles)[:, None, :]
    first = vectors[..., :half]
    second = vectors[..., half:]
    return jnp.concatenate(
        [first * cosine - second * sine, second * cosine + first * sine], axis=-1
    )


def merge_pair(earlier, later):
    peak_a, total_a, summed_a = earlier
    peak_b, total_b, summed_b = later
    peak = jnp.maximum(peak_a, peak_b)
    factor_a = jnp.exp(peak_a - peak)
    factor_b = jnp.exp(peak_b - peak)
    return (
        peak,
        total_a * factor_a + total_b * factor_b,
        summed_a * factor_a[..., None] + summed_b * factor_b[..., None],
    )


def attend(query, keys, values, new_keys, new_values, live, fresh_live):
    batch, heads, group, width = query.shape
    count = keys.shape[1]
    scale = width ** (-0.5)
    key_four = keys.reshape(batch, count, heads, width)
    value_four = values.reshape(batch, count, heads, width)
    cached = (
        jnp.einsum("bkgd,btkd->bkgt", query, key_four, preferred_element_type=jnp.float32) * scale
    )
    fresh = (
        jnp.einsum("bkgd,bskd->bkgs", query, new_keys, preferred_element_type=jnp.float32) * scale
    )
    live_mask = live[:, None, None, :]
    fresh_mask = fresh_live[None, None, None, :]
    cached = jnp.where(live_mask, cached, NEGATIVE)
    fresh = jnp.where(fresh_mask, fresh, NEGATIVE)
    local_peak = jnp.maximum(cached.max(-1), fresh.max(-1))
    flat_width = heads * group * width
    weight_cached = jnp.where(live_mask, jnp.exp(cached - local_peak[..., None]), 0.0)
    weight_fresh = jnp.where(fresh_mask, jnp.exp(fresh - local_peak[..., None]), 0.0)
    total = weight_cached.sum(-1) + weight_fresh.sum(-1)
    summed = jnp.einsum(
        "bkgt,btkd->bkgd",
        weight_cached.astype(jnp.bfloat16),
        value_four,
        preferred_element_type=jnp.float32,
    )
    summed = summed + jnp.einsum(
        "bkgs,bskd->bkgd",
        weight_fresh.astype(jnp.bfloat16),
        new_values,
        preferred_element_type=jnp.float32,
    )
    total, summed = (total, summed)
    peak, total, summed = joined_all((local_peak, total, summed), SEQ, merge_pair)
    return (summed / total[..., None]).reshape(batch, flat_width).astype(jnp.bfloat16)


def body(
    thinker_input,
    thinker_gain,
    thinker_qkv,
    thinker_out,
    talker_proj,
    code_table,
    talker_gain,
    talker_qkv,
    talker_out,
    text_keys,
    text_values,
    audio_keys,
    audio_values,
    text_len,
    audio_len,
    text_pos,
    audio_pos,
    code_ids,
):
    steps = thinker_input.shape[0]
    batch = thinker_input.shape[1]
    index = lax.axis_index(SEQ)
    shards = lax.axis_size(SEQ)
    text_kv = HK * HD
    audio_q = AHQ * AHD
    audio_kv = AHK * AHD
    text_count = text_keys.shape[1]
    audio_count = audio_keys.shape[1]
    text_live = (index * text_count + jnp.arange(text_count))[None, :] < text_len[:, None]
    audio_live = (index * audio_count + jnp.arange(audio_count))[None, :] < audio_len[:, None]
    table_rows = code_table.shape[0]
    table_ids = index * table_rows + jnp.arange(table_rows)
    feature_rows = thinker_qkv.shape[0]
    output_rows = thinker_out.shape[0]
    bridge_rows = talker_proj.shape[0]
    talker_cols = talker_out.shape[1] // shards
    out_slice = lax.dynamic_slice_in_dim(talker_out, index * talker_cols, talker_cols, 1)
    new_text_keys = jnp.zeros((batch, steps, HK, HD), jnp.bfloat16)
    new_text_values = jnp.zeros((batch, steps, HK, HD), jnp.bfloat16)
    new_audio_keys = jnp.zeros((batch, steps, AHK, AHD), jnp.bfloat16)
    new_audio_values = jnp.zeros((batch, steps, AHK, AHD), jnp.bfloat16)
    thinker_list = []
    talker_list = []
    for step in range(steps):
        fresh_live = (jnp.arange(steps) <= step) & (index == 0)
        inputs = thinker_input[step].astype(jnp.float32)
        scaled = (inputs * thinker_gain).astype(jnp.bfloat16)
        mine_scaled = lax.dynamic_slice_in_dim(scaled, index * feature_rows, feature_rows, 1)
        partial_value = jnp.dot(mine_scaled, thinker_qkv, preferred_element_type=jnp.float32)
        squares = jnp.sum(inputs * inputs, axis=-1)
        projected = by_axis(partial_value, SEQ)
        projected = projected * lax.rsqrt(squares / D + EPSILON)[:, None]
        query = rotate(projected[:, :D].reshape(batch, HQ, HD), text_pos[:, step]).astype(
            jnp.bfloat16
        )
        key = rotate(
            projected[:, D : D + text_kv].reshape(batch, HK, HD), text_pos[:, step]
        ).astype(jnp.bfloat16)
        value = projected[:, D + text_kv :].reshape(batch, HK, HD).astype(jnp.bfloat16)
        new_text_keys = new_text_keys.at[:, step].set(key)
        new_text_values = new_text_values.at[:, step].set(value)
        attended = attend(
            query.reshape(batch, HK, HQ // HK, HD),
            text_keys,
            text_values,
            new_text_keys,
            new_text_values,
            text_live,
            fresh_live,
        )
        mine_attended = lax.dynamic_slice_in_dim(attended, index * output_rows, output_rows, 1)
        contribution = over_pieces(
            jnp.dot(mine_attended, thinker_out, preferred_element_type=jnp.float32), SEQ
        )
        hidden = (inputs + contribution).astype(jnp.bfloat16)
        thinker_list.append(hidden)
        picked = (code_ids[:, step][:, None] == table_ids[None, :]).astype(jnp.bfloat16)
        mine_hidden = lax.dynamic_slice_in_dim(hidden, index * bridge_rows, bridge_rows, 1)
        pieces = jnp.dot(mine_hidden, talker_proj, preferred_element_type=jnp.float32) + jnp.dot(
            picked, code_table, preferred_element_type=jnp.float32
        )
        talker_in = taken_together(pieces, SEQ)
        normed = (
            talker_in
            * lax.rsqrt(jnp.sum(talker_in * talker_in, axis=-1, keepdims=True) / TD + EPSILON)
            * talker_gain
        ).astype(jnp.bfloat16)
        spoken = jnp.dot(normed, talker_qkv, preferred_element_type=jnp.float32)
        audio_query = rotate(
            spoken[:, :audio_q].reshape(batch, AHQ, AHD), audio_pos[:, step]
        ).astype(jnp.bfloat16)
        audio_key = rotate(
            spoken[:, audio_q : audio_q + audio_kv].reshape(batch, AHK, AHD), audio_pos[:, step]
        ).astype(jnp.bfloat16)
        audio_value = spoken[:, audio_q + audio_kv :].reshape(batch, AHK, AHD).astype(jnp.bfloat16)
        new_audio_keys = new_audio_keys.at[:, step].set(audio_key)
        new_audio_values = new_audio_values.at[:, step].set(audio_value)
        heard = attend(
            audio_query.reshape(batch, AHK, AHQ // AHK, AHD),
            audio_keys,
            audio_values,
            new_audio_keys,
            new_audio_values,
            audio_live,
            fresh_live,
        )
        residual = lax.dynamic_slice_in_dim(talker_in, index * talker_cols, talker_cols, 1)
        talker_list.append(
            (residual + jnp.dot(heard, out_slice, preferred_element_type=jnp.float32)).astype(
                jnp.bfloat16
            )
        )
    return (jnp.stack(thinker_list), jnp.stack(talker_list))


def solution(mesh):
    finer = Mesh(
        mesh.devices.reshape(mesh.shape["grp"], 8, 4, 2), ("grp", "seq_0", "seq_1", "seq_2")
    )
    placed = (
        P(None, "grp", None),
        P(),
        P(SEQ, None),
        P(SEQ, None),
        P(SEQ, None),
        P(SEQ, None),
        P(),
        P(),
        P(),
        P("grp", SEQ, None),
        P("grp", SEQ, None),
        P("grp", SEQ, None),
        P("grp", SEQ, None),
        P("grp"),
        P("grp"),
        P("grp", None),
        P("grp", None),
        P("grp", None),
    )
    return jax.shard_map(
        body,
        mesh=finer,
        in_specs=placed,
        out_specs=(P(None, "grp", None), P(None, "grp", SEQ)),
        check_vma=False,
    )
```

profile of v0, /device:TPU:1, one launch (start us, length us, event | category | flops | bytes accessed | tf_op | source)
XLA Modules:
  0.0 944.4 jit_solution(8341873503172578787)
XLA Ops:
  9.2 2.0 fusion.441
  11.2 1.9 fusion.438
  13.1 1.9 fusion.439
  15.1 1.9 fusion.440
  19.3 71.3 %all-reduce.59.cloned.1.call-done = (f32[8,4608]{1,0:T(8,128)}, f32[8,4608]{1,0:T(8,128)}, f32[8,4608]{1,0:T(8,128)}, f32[8,4608]{1,0:T(8,128)}) async-done(((f32[8,4608]{1,0:T(8,128)}, f32[8,4608]{1,0:T(8,128)}, f32[8,4608]{1,0:T(8,128)}, f32[8,4608]{1,0:T(8,128)}), (f32[8,4608]{1,0:T(8,128)}, f32[8,4608]{1,0:T(8,128)}, f32[8,4608]{1,0:T(8,128)}, f32[8,4608]{1,0:T(8,128)})) %all-reduce.59.cloned.1.call-update) | async-done | bytes 589840 | tf_op jit(solution)/shard_map/psum | solution.py:63
  91.8 51.0 %all-reduce.61.cloned.1.call-done = (f32[8,4608]{1,0:T(8,128)}, f32[8,4608]{1,0:T(8,128)}, f32[8,4608]{1,0:T(8,128)}, f32[8,4608]{1,0:T(8,128)}) async-done(((f32[8,4608]{1,0:T(8,128)}, f32[8,4608]{1,0:T(8,128)}, f32[8,4608]{1,0:T(8,128)}, f32[8,4608]{1,0:T(8,128)}), (f32[8,4608]{1,0:T(8,128)}, f32[8,4608]{1,0:T(8,128)}, f32[8,4608]{1,0:T(8,128)}, f32[8,4608]{1,0:T(8,128)})) %all-reduce.61.cloned.1.call-update) | async-done | bytes 589840 | tf_op jit(solution)/shard_map/psum | solution.py:63
  143.7 35.0 %all-reduce.63.cloned.1.call-done = (f32[8,4608]{1,0:T(8,128)}, f32[8,4608]{1,0:T(8,128)}, f32[8,4608]{1,0:T(8,128)}, f32[8,4608]{1,0:T(8,128)}) async-done(((f32[8,4608]{1,0:T(8,128)}, f32[8,4608]{1,0:T(8,128)}, f32[8,4608]{1,0:T(8,128)}, f32[8,4608]{1,0:T(8,128)}), (f32[8,4608]{1,0:T(8,128)}, f32[8,4608]{1,0:T(8,128)}, f32[8,4608]{1,0:T(8,128)}, f32[8,4608]{1,0:T(8,128)})) %all-reduce.63.cloned.1.call-update) | async-done | bytes 589840 | tf_op jit(solution)/shard_map/psum | solution.py:63
  187.1 2.6 fusion.736
  196.1 1.7 fusion.5
  206.6 2.1 fusion.740
  208.6 1.8 fusion.741
  212.6 2.1 fusion.742
  214.6 1.8 fusion.743
  217.6 1.9 fusion.156
  223.6 20.1 %all-gather.31 = bf16[8,228,128]{2,1,0:T(8,128)(2,1)S(1)} all-gather(bf16[1,228,128]{2,1,0:T(8,128)(2,1)S(1)} %maximum_bitcast_fusion.3), channel_id=6, replica_groups=mesh['grp'=4,'seq_0'=8,'seq_1'=4,'seq_2'=2] {'seq_0'}, dimensions={0}, use_global_device_ids=true | all-gather | bytes 525312 | tf_op jit(solution)/shard_map/all_gather | solution.py:33
  244.4 9.9 %all-gather.32 = bf16[4,228,128]{2,1,0:T(8,128)(2,1)S(1)} all-gather(bf16[1,228,128]{2,1,0:T(8,128)(2,1)S(1)} %maximum_bitcast_fusion.4), channel_id=7, replica_groups=mesh['grp'=4,'seq_0'=8,'seq_1'=4,'seq_2'=2] {'seq_1'}, dimensions={0}, use_global_device_ids=true | all-gather | bytes 291840 | tf_op jit(solution)/shard_map/all_gather | solution.py:33
  254.7 10.8 %all-gather.33 = bf16[2,228,128]{2,1,0:T(8,128)(2,1)S(1)} all-gather(bf16[1,228,128]{2,1,0:T(8,128)(2,1)S(1)} %maximum_bitcast_fusion.5), channel_id=8, replica_groups=mesh['grp'=4,'seq_0'=8,'seq_1'=4,'seq_2'=2] {'seq_2'}, dimensions={0}, use_global_device_ids=true | all-gather | bytes 175104 | tf_op jit(solution)/shard_map/all_gather | solution.py:33
  287.8 2.3 fusion.4
  296.1 20.7 %all-gather.28 = bf16[8,228,128]{2,1,0:T(8,128)(2,1)S(1)} all-gather(bf16[1,228,128]{2,1,0:T(8,128)(2,1)S(1)} %maximum_bitcast_fusion), channel_id=2, replica_groups=mesh['grp'=4,'seq_0'=8,'seq_1'=4,'seq_2'=2] {'seq_0'}, dimensions={0}, use_global_device_ids=true | all-gather | bytes 525312 | tf_op jit(solution)/shard_map/all_gather | solution.py:33
  317.5 10.0 %all-gather.29 = bf16[4,228,128]{2,1,0:T(8,128)(2,1)S(1)} all-gather(bf16[1,228,128]{2,1,0:T(8,128)(2,1)S(1)} %maximum_bitcast_fusion.1), channel_id=3, replica_groups=mesh['grp'=4,'seq_0'=8,'seq_1'=4,'seq_2'=2] {'seq_1'}, dimensions={0}, use_global_device_ids=true | all-gather | bytes 291840 | tf_op jit(solution)/shard_map/all_gather | solution.py:33
  327.9 9.2 all-gather.30
  362.8 1.7 fusion.6
  367.0 19.9 %all-gather.34 = bf16[8,228,128]{2,1,0:T(8,128)(2,1)S(1)} all-gather(bf16[1,228,128]{2,1,0:T(8,128)(2,1)S(1)} %maximum_bitcast_fusion.6), channel_id=10, replica_groups=mesh['grp'=4,'seq_0'=8,'seq_1'=4,'seq_2'=2] {'seq_0'}, dimensions={0}, use_global_device_ids=true | all-gather | bytes 525312 | tf_op jit(solution)/shard_map/all_gather | solution.py:33
  387.6 10.5 %all-gather.35 = bf16[4,228,128]{2,1,0:T(8,128)(2,1)S(1)} all-gather(bf16[1,228,128]{2,1,0:T(8,128)(2,1)S(1)} %maximum_bitcast_fusion.7), channel_id=11, replica_groups=mesh['grp'=4,'seq_0'=8,'seq_1'=4,'seq_2'=2] {'seq_1'}, dimensions={0}, use_global_device_ids=true | all-gather | bytes 291840 | tf_op jit(solution)/shard_map/all_gather | solution.py:33
  398.5 9.3 all-gather.36
  420.3 1.7 fusion.7
  422.1 22.6 %all-gather.37 = bf16[8,228,128]{2,1,0:T(8,128)(2,1)S(1)} all-gather(bf16[1,228,128]{2,1,0:T(8,128)(2,1)S(1)} %maximum_bitcast_fusion.9), channel_id=14, replica_groups=mesh['grp'=4,'seq_0'=8,'seq_1'=4,'seq_2'=2] {'seq_0'}, dimensions={0}, use_global_device_ids=true | all-gather | bytes 525312 | tf_op jit(solution)/shard_map/all_gather | solution.py:33
  445.4 9.3 all-gather.38
  455.1 8.2 all-gather.39
  470.8 3.5 bitcast_reduce_fusion.2
  476.8 8.4 all-to-all-start.1
  485.1 3.4 bitcast_reduce_fusion.3
  490.3 50.1 %all-to-all-done.1 = f32[64,8,896]{2,1,0:T(8,128)} async-done(((f32[64,8,896]{2,1,0:T(8,128)}), f32[64,8,896]{2,1,0:T(8,128)}, u32[]{:S(2)}, u32[]{:S(2)}) %all-to-all-start.1) | async-done | bytes 1835040 | tf_op jit(solution)/shard_map/all_to_all | solution.py:72
  541.8 9.8 %all-to-all-start = ((f32[64,8,896]{2,1,0:T(8,128)}), f32[64,8,896]{2,1,0:T(8,128)}, u32[]{:S(2)}, u32[]{:S(2)}) async-start(f32[64,8,896]{2,1,0:T(8,128)} %broadcast_in_dim.197), calls=%async_computation | async-start | bytes 3670016 | tf_op jit(solution)/shard_map/all_to_all | solution.py:72
  551.7 3.4 bitcast_reduce_fusion.1
  556.8 43.5 %all-to-all-done = f32[64,8,896]{2,1,0:T(8,128)} async-done(((f32[64,8,896]{2,1,0:T(8,128)}), f32[64,8,896]{2,1,0:T(8,128)}, u32[]{:S(2)}, u32[]{:S(2)}) %all-to-all-start) | async-done | bytes 1835040 | tf_op jit(solution)/shard_map/all_to_all | solution.py:72
  601.7 6.8 all-to-all-start.2
  608.5 56.5 %all-gather.63.cloned.1.call-done = f32[512,3584]{1,0:T(8,128)} async-done(((f32[8,3584]{1,0:T(8,128)}), f32[512,3584]{1,0:T(8,128)}) %all-gather.63.cloned.1.call-update) | async-done | bytes 7340048 | tf_op jit(solution)/shard_map/all_gather | solution.py:67
  665.0 3.4 bitcast_reduce_fusion
  676.1 10.4 %all-to-all-start.3 = ((f32[64,8,896]{2,1,0:T(8,128)}), f32[64,8,896]{2,1,0:T(8,128)}, u32[]{:S(2)}, u32[]{:S(2)}) async-start(f32[64,8,896]{2,1,0:T(8,128)} %broadcast_in_dim.208), calls=%async_computation.3 | async-start | bytes 3670016 | tf_op jit(solution)/shard_map/all_to_all | solution.py:72
  686.5 1.7 reduce_sum.324
  688.4 3.2 fusion.359
  691.6 3.0 fusion.358
  695.5 35.2 %all-to-all-done.3 = f32[64,8,896]{2,1,0:T(8,128)} async-done(((f32[64,8,896]{2,1,0:T(8,128)}), f32[64,8,896]{2,1,0:T(8,128)}, u32[]{:S(2)}, u32[]{:S(2)}) %all-to-all-start.3) | async-done | bytes 1835040 | tf_op jit(solution)/shard_map/all_to_all | solution.py:72
  732.5 3.1 fusion.361
  742.4 2.6 fusion.748
  745.0 1.7 fusion.749
  748.4 2.1 fusion.750
  753.1 2.3 fusion.38
  755.4 2.3 fusion.36
  758.4 2.3 fusion.34
  762.0 1.7 fusion.32
  769.6 19.8 %all-gather.49 = bf16[8,98,128]{2,1,0:T(8,128)(2,1)S(1)} all-gather(bf16[1,98,128]{2,1,0:T(8,128)(2,1)S(1)} %maximum_bitcast_fusion.21), channel_id=27, replica_groups=mesh['grp'=4,'seq_0'=8,'seq_1'=4,'seq_2'=2] {'seq_0'}, dimensions={0}, use_global_device_ids=true | all-gather | bytes 225792 | tf_op jit(solution)/shard_map/all_gather | solution.py:33
  789.8 9.4 all-gather.50
  799.4 11.2 %all-gather.51 = bf16[2,98,128]{2,1,0:T(8,128)(2,1)S(1)} all-gather(bf16[1,98,128]{2,1,0:T(8,128)(2,1)S(1)} %maximum_bitcast_fusion.23), channel_id=29, replica_groups=mesh['grp'=4,'seq_0'=8,'seq_1'=4,'seq_2'=2] {'seq_2'}, dimensions={0}, use_global_device_ids=true | all-gather | bytes 75264 | tf_op jit(solution)/shard_map/all_gather | solution.py:33
  810.9 18.7 %all-gather.46 = bf16[8,98,128]{2,1,0:T(8,128)(2,1)S(1)} all-gather(bf16[1,98,128]{2,1,0:T(8,128)(2,1)S(1)} %maximum_bitcast_fusion.18), channel_id=24, replica_groups=mesh['grp'=4,'seq_0'=8,'seq_1'=4,'seq_2'=2] {'seq_0'}, dimensions={0}, use_global_device_ids=true | all-gather | bytes 225792 | tf_op jit(solution)/shard_map/all_gather | solution.py:33
  829.9 9.1 all-gather.47
  839.3 10.8 %all-gather.48 = bf16[2,98,128]{2,1,0:T(8,128)(2,1)S(1)} all-gather(bf16[1,98,128]{2,1,0:T(8,128)(2,1)S(1)} %maximum_bitcast_fusion.20), channel_id=26, replica_groups=mesh['grp'=4,'seq_0'=8,'seq_1'=4,'seq_2'=2] {'seq_2'}, dimensions={0}, use_global_device_ids=true | all-gather | bytes 75264 | tf_op jit(solution)/shard_map/all_gather | solution.py:33
  851.7 18.7 %all-gather.40 = bf16[8,98,128]{2,1,0:T(8,128)(2,1)S(1)} all-gather(bf16[1,98,128]{2,1,0:T(8,128)(2,1)S(1)} %maximum_bitcast_fusion.12), channel_id=18, replica_groups=mesh['grp'=4,'seq_0'=8,'seq_1'=4,'seq_2'=2] {'seq_0'}, dimensions={0}, use_global_device_ids=true | all-gather | bytes 225792 | tf_op jit(solution)/shard_map/all_gather | solution.py:33
  870.7 9.1 all-gather.41
  880.1 10.8 %all-gather.42 = bf16[2,98,128]{2,1,0:T(8,128)(2,1)S(1)} all-gather(bf16[1,98,128]{2,1,0:T(8,128)(2,1)S(1)} %maximum_bitcast_fusion.14), channel_id=20, replica_groups=mesh['grp'=4,'seq_0'=8,'seq_1'=4,'seq_2'=2] {'seq_2'}, dimensions={0}, use_global_device_ids=true | all-gather | bytes 75264 | tf_op jit(solution)/shard_map/all_gather | solution.py:33
  891.2 18.9 %all-gather.43 = bf16[8,98,128]{2,1,0:T(8,128)(2,1)S(1)} all-gather(bf16[1,98,128]{2,1,0:T(8,128)(2,1)S(1)} %maximum_bitcast_fusion.15), channel_id=21, replica_groups=mesh['grp'=4,'seq_0'=8,'seq_1'=4,'seq_2'=2] {'seq_0'}, dimensions={0}, use_global_device_ids=true | all-gather | bytes 225792 | tf_op jit(solution)/shard_map/all_gather | solution.py:33
  910.5 9.1 all-gather.44
  919.8 10.8 %all-gather.45 = bf16[2,98,128]{2,1,0:T(8,128)(2,1)S(1)} all-gather(bf16[1,98,128]{2,1,0:T(8,128)(2,1)S(1)} %maximum_bitcast_fusion.17), channel_id=23, replica_groups=mesh['grp'=4,'seq_0'=8,'seq_1'=4,'seq_2'=2] {'seq_2'}, dimensions={0}, use_global_device_ids=true | all-gather | bytes 75264 | tf_op jit(solution)/shard_map/all_gather | solution.py:33
  (684 shorter events, 165.3 us)
Async XLA Ops:
  7.2 927.4 %copy-start = (bf16[1536,896]{1,0:T(8,128)(2,1)S(1)}, bf16[1536,896]{1,0:T(8,128)(2,1)}, u32[]{:S(2)}) copy-start(bf16[1536,896]{1,0:T(8,128)(2,1)} %param.58) | copy-start | bytes 8257540
  7.2 84.0 %copy-start.48 = (s32[8]{0:T(128)S(1)}, s32[8]{0:T(128)}, u32[]{:S(2)}) copy-start(s32[8]{0:T(128)} %param.64) | copy-start | bytes 100
  7.2 84.0 %copy-start.49 = (s32[8]{0:T(128)S(1)}, s32[8]{0:T(128)}, u32[]{:S(2)}) copy-start(s32[8]{0:T(128)} %param.63) | copy-start | bytes 100
  7.2 84.6 %copy-start.46 = (s32[8,4]{0,1:T(4,128)S(1)}, s32[8,4]{0,1:T(4,128)}, u32[]{:S(2)}) copy-start(s32[8,4]{0,1:T(4,128)} %param.65) | copy-start | bytes 388
  7.2 135.7 %copy-start.47 = (s32[8,4]{0,1:T(4,128)S(1)}, s32[8,4]{0,1:T(4,128)}, u32[]{:S(2)}) copy-start(s32[8,4]{0,1:T(4,128)} %param.66) | copy-start | bytes 388
  7.2 83.3 %all-reduce.59.cloned.1.call-start = ((), (), s32[]{:S(2)}) async-start(), calls=%async_computation.8 | async-start | bytes 1179648 | tf_op jit(solution)/shard_map/psum | solution.py:63
  8.4 171.4 %copy-start.23 = (f32[8,3584]{1,0:T(8,128)}, f32[8,3584]{1,0:T(8,128)S(1)}, u32[]{:S(2)}) copy-start(f32[8,3584]{1,0:T(8,128)S(1)} %get-tuple-element.544) | copy-start | bytes 344068
  8.4 176.4 %copy-start.21 = (f32[8,3584]{1,0:T(8,128)}, f32[8,3584]{1,0:T(8,128)S(1)}, u32[]{:S(2)}) copy-start(f32[8,3584]{1,0:T(8,128)S(1)} %get-tuple-element.545) | copy-start | bytes 344068
  8.4 176.4 %copy-start.22 = (f32[8,3584]{1,0:T(8,128)}, f32[8,3584]{1,0:T(8,128)S(1)}, u32[]{:S(2)}) copy-start(f32[8,3584]{1,0:T(8,128)S(1)} %get-tuple-element.543) | copy-start | bytes 344068
  8.4 178.7 %copy-start.20 = (f32[8,3584]{1,0:T(8,128)}, f32[8,3584]{1,0:T(8,128)S(1)}, u32[]{:S(2)}) copy-start(f32[8,3584]{1,0:T(8,128)S(1)} %get-tuple-element.542) | copy-start | bytes 344068
  17.0 125.7 %all-reduce.61.cloned.1.call-start = ((), (), s32[]{:S(2)}) async-start(), calls=%async_computation.9 | async-start | bytes 1179648 | tf_op jit(solution)/shard_map/psum | solution.py:63
  90.6 88.2 %all-reduce.63.cloned.1.call-start = ((), (), s32[]{:S(2)}) async-start(), calls=%async_computation.10 | async-start | bytes 1179648 | tf_op jit(solution)/shard_map/psum | solution.py:63
  142.8 328.0 %all-gather.59.cloned.1.call-start = ((), (), s32[]{:S(2)}) async-start(), calls=%async_computation.5 | async-start | bytes 7454720 | tf_op jit(solution)/shard_map/all_gather | solution.py:67
  142.8 44.2 %copy-start.40 = (pred[4]{0:T(512)(128)(4,1)}, pred[4]{0:T(512)(128)(4,1)S(1)}, u32[]{:S(2)}) copy-start(pred[4]{0:T(512)(128)(4,1)S(1)} %compare_and_fusion.3) | copy-start | bytes 16
  178.7 11.0 %copy-start.1 = (bf16[8,128,512]{2,1,0:T(8,128)(2,1)S(1)}, bf16[8,128,512]{2,1,0:T(8,128)(2,1)}, u32[]{:S(2)}) copy-start(bf16[8,128,512]{2,1,0:T(8,128)(2,1)} %param.59) | copy-start | bytes 3145732
  179.8 18.6 %copy-start.28 = (f32[8,64]{1,0:T(8,128)S(1)}, f32[8,64]{1,0:T(8,128)}, u32[]{:S(2)}) copy-start(f32[8,64]{1,0:T(8,128)} %get-tuple-element.752) | copy-start | bytes 6148
  179.8 18.6 %copy-start.29 = (f32[8,64]{1,0:T(8,128)S(1)}, f32[8,64]{1,0:T(8,128)}, u32[]{:S(2)}) copy-start(f32[8,64]{1,0:T(8,128)} %get-tuple-element.753) | copy-start | bytes 6148
  181.9 0.7 copy-start.8
  183.6 3.5 copy-start.7
  184.3 14.1 %copy-start.19 = (bf16[8,1,4,128]{3,1,2,0:T(2,128)(2,1)}, bf16[8,1,4,128]{3,1,2,0:T(2,128)(2,1)S(1)}, u32[]{:S(2)}) copy-start(bf16[8,1,4,128]{3,1,2,0:T(2,128)(2,1)S(1)} %copy.348) | copy-start | bytes 24580
  190.5 9.5 %copy-start.6 = (f32[8,4,7,128]{3,2,1,0:T(8,128)}, f32[8,4,7,128]{3,2,1,0:T(8,128)S(1)}, u32[]{:S(2)}) copy-start(f32[8,4,7,128]{3,2,1,0:T(8,128)S(1)} %get-tuple-element.771) | copy-start | bytes 344068
  193.0 7.0 copy-start.17
  193.8 11.4 %copy-start.9 = (bf16[8,4,4,128]{3,1,2,0:T(4,128)(2,1)}, bf16[8,4,4,128]{3,1,2,0:T(4,128)(2,1)S(1)}, u32[]{:S(2)}) copy-start(bf16[8,4,4,128]{3,1,2,0:T(4,128)(2,1)S(1)} %scatter.59) | copy-start | bytes 98308
  200.7 82.9 %copy-start.2 = (bf16[56,3584]{1,0:T(8,128)(2,1)S(1)}, bf16[56,3584]{1,0:T(8,128)(2,1)}, u32[]{:S(2)}) copy-start(bf16[56,3584]{1,0:T(8,128)(2,1)} %param.53) | copy-start | bytes 1204228
  204.5 82.1 %copy-start.41 = (pred[4]{0:T(512)(128)(4,1)S(1)}, pred[4]{0:T(512)(128)(4,1)}, u32[]{:S(2)}) copy-start(pred[4]{0:T(512)(128)(4,1)} %copy-done.40) | copy-start | bytes 16
  285.2 199.9 %all-gather.57.cloned.1.call-start = ((), (), s32[]{:S(2)}) async-start(), calls=%async_computation.4 | async-start | bytes 7454720 | tf_op jit(solution)/shard_map/all_gather | solution.py:67
  290.1 69.7 %copy-start.10 = (bf16[8,4,4,128]{3,1,2,0:T(4,128)(2,1)S(1)}, bf16[8,4,4,128]{3,1,2,0:T(4,128)(2,1)}, u32[]{:S(2)}) copy-start(bf16[8,4,4,128]{3,1,2,0:T(4,128)(2,1)} %copy-done.9) | copy-start | bytes 98308
  290.1 71.8 %copy-start.16 = (f32[8,4,7]{2,1,0:T(4,128)S(1)}, f32[8,4,7]{2,1,0:T(4,128)}, u32[]{:S(2)}) copy-start(f32[8,4,7]{2,1,0:T(4,128)} %get-tuple-element.488) | copy-start | bytes 2692
  290.1 71.8 %copy-start.18 = (f32[8,4,7,4]{2,3,1,0:T(4,128)S(1)}, f32[8,4,7,4]{2,3,1,0:T(4,128)}, u32[]{:S(2)}) copy-start(f32[8,4,7,4]{2,3,1,0:T(4,128)} %get-tuple-element.777) | copy-start | bytes 10756
  327.9 90.2 %copy-start.15 = (f32[8,4,7]{2,1,0:T(4,128)S(1)}, f32[8,4,7]{2,1,0:T(4,128)}, u32[]{:S(2)}) copy-start(f32[8,4,7]{2,1,0:T(4,128)} %copy-done.14) | copy-start | bytes 2692
  337.1 0.6 copy-start.13
  358.4 193.3 %all-gather.61.cloned.1.call-start = ((), (), s32[]{:S(2)}) async-start(), calls=%async_computation.6 | async-start | bytes 7454720 | tf_op jit(solution)/shard_map/all_gather | solution.py:67
  364.5 53.5 %copy-start.38 = (bf16[8,4,7]{2,1,0:T(4,128)(2,1)S(1)}, bf16[8,4,7]{2,1,0:T(4,128)(2,1)}, u32[]{:S(2)}) copy-start(bf16[8,4,7]{2,1,0:T(4,128)(2,1)} %get-tuple-element.520) | copy-start | bytes 1348
  364.5 54.6 %copy-start.25 = (f32[8,4,7]{2,1,0:T(4,128)S(1)}, f32[8,4,7]{2,1,0:T(4,128)}, u32[]{:S(2)}) copy-start(f32[8,4,7]{2,1,0:T(4,128)} %get-tuple-element.209) | copy-start | bytes 2692
  417.1 247.9 %all-gather.63.cloned.1.call-start = ((), (), s32[]{:S(2)}) async-start(), calls=%async_computation.7 | async-start | bytes 7454720 | tf_op jit(solution)/shard_map/all_gather | solution.py:67
  464.2 10.1 %copy-start.5 = (bf16[56,896]{1,0:T(8,128)(2,1)S(1)}, bf16[56,896]{1,0:T(8,128)(2,1)}, u32[]{:S(2)}) copy-start(bf16[56,896]{1,0:T(8,128)(2,1)} %param.54) | copy-start | bytes 301060
  464.9 10.3 %copy-start.3 = (bf16[132,896]{1,0:T(8,128)(2,1)S(1)}, bf16[132,896]{1,0:T(8,128)(2,1)}, u32[]{:S(2)}) copy-start(bf16[132,896]{1,0:T(8,128)(2,1)} %param.55) | copy-start | bytes 709636
  476.8 63.7 %all-to-all-start.1 = ((f32[64,8,896]{2,1,0:T(8,128)}), f32[64,8,896]{2,1,0:T(8,128)}, u32[]{:S(2)}, u32[]{:S(2)}) async-start(f32[64,8,896]{2,1,0:T(8,128)} %broadcast_in_dim.204), calls=%async_computation.1 | async-start | bytes 3670016 | tf_op jit(solution)/shard_map/all_to_all | solution.py:72
  488.6 0.6 copy-start.11
  541.8 58.5 %all-to-all-start = ((f32[64,8,896]{2,1,0:T(8,128)}), f32[64,8,896]{2,1,0:T(8,128)}, u32[]{:S(2)}, u32[]{:S(2)}) async-start(f32[64,8,896]{2,1,0:T(8,128)} %broadcast_in_dim.197), calls=%async_computation | async-start | bytes 3670016 | tf_op jit(solution)/shard_map/all_to_all | solution.py:72
  555.1 0.6 copy-start.12
  601.7 73.1 %all-to-all-start.2 = ((f32[64,8,896]{2,1,0:T(8,128)}), f32[64,8,896]{2,1,0:T(8,128)}, u32[]{:S(2)}, u32[]{:S(2)}) async-start(f32[64,8,896]{2,1,0:T(8,128)} %broadcast_in_dim.206), calls=%async_computation.2 | async-start | bytes 3670016 | tf_op jit(solution)/shard_map/all_to_all | solution.py:72
  608.5 61.0 %copy-start.4 = (bf16[4,8,3584]{2,1,0:T(8,128)(2,1)S(1)}, bf16[4,8,3584]{2,1,0:T(8,128)(2,1)}, u32[]{:S(2)}) copy-start(bf16[4,8,3584]{2,1,0:T(8,128)(2,1)} %param.50) | copy-start | bytes 688132
  672.9 15.5 %copy-start.24 = (f32[896]{0:T(1024)S(1)}, f32[896]{0:T(1024)}, u32[]{:S(2)}) copy-start(f32[896]{0:T(1024)} %param.56) | copy-start | bytes 10756
  676.1 54.5 %all-to-all-start.3 = ((f32[64,8,896]{2,1,0:T(8,128)}), f32[64,8,896]{2,1,0:T(8,128)}, u32[]{:S(2)}, u32[]{:S(2)}) async-start(f32[64,8,896]{2,1,0:T(8,128)} %broadcast_in_dim.208), calls=%async_computation.3 | async-start | bytes 3670016 | tf_op jit(solution)/shard_map/all_to_all | solution.py:72
  686.5 8.1 slice-start
  688.4 6.3 slice-start.1
  695.4 40.3 %copy-start.36 = (f32[8,64]{1,0:T(8,128)S(1)}, f32[8,64]{1,0:T(8,128)}, u32[]{:S(2)}) copy-start(f32[8,64]{1,0:T(8,128)} %get-tuple-element.758) | copy-start | bytes 6148
  695.4 40.3 %copy-start.37 = (f32[8,64]{1,0:T(8,128)S(1)}, f32[8,64]{1,0:T(8,128)}, u32[]{:S(2)}) copy-start(f32[8,64]{1,0:T(8,128)} %get-tuple-element.759) | copy-start | bytes 6148
  695.4 40.6 %copy-start.34 = (f32[8,64]{1,0:T(8,128)S(1)}, f32[8,64]{1,0:T(8,128)}, u32[]{:S(2)}) copy-start(f32[8,64]{1,0:T(8,128)} %get-tuple-element.756) | copy-start | bytes 6148
  695.4 40.6 %copy-start.35 = (f32[8,64]{1,0:T(8,128)S(1)}, f32[8,64]{1,0:T(8,128)}, u32[]{:S(2)}) copy-start(f32[8,64]{1,0:T(8,128)} %get-tuple-element.757) | copy-start | bytes 6148
  695.4 42.0 %copy-start.45 = (pred[8,128]{1,0:T(8,128)(4,1)S(1)}, pred[8,128]{1,0:T(8,128)(4,1)}, u32[]{:S(2)}) copy-start(pred[8,128]{1,0:T(8,128)(4,1)} %get-tuple-element.764) | copy-start | bytes 3076
  732.3 5.1 copy-start.50
  732.3 7.3 copy-start.43
  732.3 8.2 copy-start.32
  732.4 8.2 copy-start.33
  732.5 12.5 %copy-start.42 = (pred[4]{0:T(512)(128)(4,1)S(1)}, pred[4]{0:T(512)(128)(4,1)}, u32[]{:S(2)}) copy-start(pred[4]{0:T(512)(128)(4,1)} %compare_and_fusion.1) | copy-start | bytes 16
  732.5 14.1 %copy-start.30 = (f32[8,64]{1,0:T(8,128)S(1)}, f32[8,64]{1,0:T(8,128)}, u32[]{:S(2)}) copy-start(f32[8,64]{1,0:T(8,128)} %get-tuple-element.734) | copy-start | bytes 6148
  732.5 14.1 %copy-start.31 = (f32[8,64]{1,0:T(8,128)S(1)}, f32[8,64]{1,0:T(8,128)}, u32[]{:S(2)}) copy-start(f32[8,64]{1,0:T(8,128)} %get-tuple-element.735) | copy-start | bytes 6148
  735.7 14.8 %copy-start.44 = (pred[4]{0:T(512)(128)(4,1)S(1)}, pred[4]{0:T(512)(128)(4,1)}, u32[]{:S(2)}) copy-start(pred[4]{0:T(512)(128)(4,1)} %compare_and_fusion) | copy-start | bytes 16
  739.5 21.2 %copy-start.26 = (f32[8,4,3,128]{3,2,1,0:T(4,128)}, f32[8,4,3,128]{3,2,1,0:T(4,128)S(1)}, u32[]{:S(2)}) copy-start(f32[8,4,3,128]{3,2,1,0:T(4,128)S(1)} %get-tuple-element.787) | copy-start | bytes 147460
  739.6 0.9 copy-start.39
  745.0 15.7 %copy-start.27 = (f32[8,4,3,128]{3,2,1,0:T(4,128)}, f32[8,4,3,128]{3,2,1,0:T(4,128)S(1)}, u32[]{:S(2)}) copy-start(f32[8,4,3,128]{3,2,1,0:T(4,128)S(1)} %get-tuple-element.791) | copy-start | bytes 147460
  748.4 13.6 %copy-start.51 = (bf16[8,128,512]{2,1,0:T(8,128)(2,1)S(1)}, bf16[8,128,512]{2,1,0:T(8,128)(2,1)}, u32[]{:S(2)}) copy-start(bf16[8,128,512]{2,1,0:T(8,128)(2,1)} %param.62) | copy-start | bytes 3145732
  (1 other events, 0.6 us)
Sparse Core Ops, SparseCore 0:
  17.2 73.3 all-reduce.58
  93.1 49.6 all-reduce.60
  145.6 33.0 all-reduce.62
  285.4 81.1 all-gather.58
  369.1 79.4 all-gather.56
  451.3 97.4 all-gather.60
  551.5 113.4 all-gather.62
where the time goes:
time: 957 us; the launch traced here: 944 us
  waiting for transfers between devices  343 us (36%)
  blocking collectives  317 us (33%)
  local copies, waits for them, and re-layouts  80.9 us (8%)
  matrix products  79.2 us (8%)
  other arithmetic  71.9 us (8%)
  starting transfers between devices  35.7 us (4%)
  between operations  17.4 us (2%)
    all_gather x24, blocking collectives, all_in_one(): both, at, found = (lax.all_gather(jnp.concatenate(lines), axis), 0, {})  317 us
    psum x3, waiting for transfers between devices, by_axis(): return functools.reduce(lax.psum, axes, shard)  157 us
    all_to_all x4, waiting for transfers between devices, copy_for_each(): lax.all_to_all(jnp.broadcast_to(shard[None], (length, *shard.shape)), axi...  129 us
    all_gather x4, waiting for transfers between devices, over_pieces(): return lax.all_gather(shard, axis).sum(0)  56.5 us
    all_to_all x4, starting transfers between devices, copy_for_each(): lax.all_to_all(jnp.broadcast_to(shard[None], (length, *shard.shape)), axi...  35.4 us
    convert_element_type x48, local copies, waits for them, and re-layouts, joined_all(): part[k].astype(own.dtype)  26.5 us
  transfers between devices with their start and end apart: 11, of which 7 were waited for; matrix products, arithmetic and copies ran while one was open for 11% of the time, Pallas kernels for 0%

commit v1 on v0

v1 whole, which is shorter than its diff:
```python
import jax
import jax.numpy as jnp
from jax import lax
from jax.experimental import pallas as pl
from jax.experimental.pallas import tpu as pltpu
from jax.sharding import PartitionSpec as P

D = 3584
HQ = 28
HK = 4
HD = 128
TD = 896
AHQ = 12
AHK = 4
AHD = 128
SEQ = "seq"
EPSILON = 1e-06
THETA = 1000000.0
NEGATIVE = -1e30
DEV = 64
ROWS = 32
BATCH = 8
STEPS = 4
FT = 56
FA = 24
CT = 14
INTERPRET = False

f32 = jnp.float32
bf16 = jnp.bfloat16
VM = pltpu.VMEM


def call(kernel, outs, scratch=(), name=None, scalars=1, count=0):
    specs = [pl.BlockSpec(memory_space=pltpu.SMEM)] * scalars + [pl.BlockSpec(memory_space=VM)] * count
    many = isinstance(outs, (tuple, list))
    return pl.pallas_call(
        kernel,
        out_shape=outs,
        in_specs=specs,
        out_specs=[pl.BlockSpec(memory_space=VM)] * len(outs) if many else pl.BlockSpec(memory_space=VM),
        scratch_shapes=list(scratch),
        name=name,
        interpret=INTERPRET,
    )


def iota(shape, axis):
    return lax.broadcasted_iota(jnp.int32, shape, axis)


def roll(x, shift):
    shift = shift % x.shape[1]
    return x if shift == 0 else pltpu.roll(x, shift, 1)


def mm(a, b):
    return jnp.dot(a, b, preferred_element_type=f32)


def pack(out_ref, block, extra, width, groups):
    span = 128 // groups
    high = ROWS // groups
    lane = iota((ROWS, 128), 1)
    for j in range(DEV):
        first, off = divmod(width * j, 128)
        n0 = min(width, 128 - off)
        tile = roll(block(first), -off)
        if n0 < width:
            tile = jnp.where(lane < n0, tile, roll(block(first + 1), n0))
        if extra is None:
            tile = jnp.where(lane < width, tile, 0.0)
        else:
            tail = extra(first)
            if n0 < width:
                tail = tail + roll(extra(first + 1), 3)
            tile = jnp.where(lane < width, tile, tail)
        out = tile[0:high]
        for g in range(1, groups):
            out = out + roll(tile[g * high : (g + 1) * high], g * span)
        out_ref[j] = out.astype(bf16)


def unpack(tile, groups):
    span = 128 // groups
    return jnp.concatenate([roll(tile, -g * span) for g in range(groups)], axis=0)


def attend(q_of, kn_of, vn_of, keys_ref, values_ref, limit, dev, group, o_ref, e_ref, width):
    high = group * ROWS
    row = iota((high, 128), 0)
    lane = iota((high, 128), 1)
    conv = row & 7
    lim = jnp.broadcast_to(limit[None], (group * STEPS, BATCH, 128)).reshape(high, 128)
    live = lane < lim
    frow = iota((high, ROWS), 0)
    fcol = iota((high, ROWS), 1)
    reach = jnp.where(dev == 0, (frow >> 3) & 3, -1)
    fresh_live = ((frow & 7) == (fcol & 7)) & ((fcol >> 3) <= reach)
    scale = HD**-0.5
    for k in range(HK):
        q = q_of(k)
        keys = keys_ref[:, :, 128 * k : 128 * k + 128].reshape(BATCH * 128, 128)
        values = values_ref[:, :, 128 * k : 128 * k + 128].reshape(BATCH * 128, 128)
        every = lax.dot_general(q, keys, (((1,), (1,)), ((), ())), preferred_element_type=f32)
        s = every[:, 0:128]
        for b in range(1, BATCH):
            s = jnp.where(conv == b, every[:, 128 * b : 128 * b + 128], s)
        f = lax.dot_general(q, kn_of(k), (((1,), (1,)), ((), ())), preferred_element_type=f32)
        s = jnp.where(live, s * scale, NEGATIVE)
        f = jnp.where(fresh_live, f * scale, NEGATIVE)
        m = jnp.maximum(jnp.max(s, axis=1, keepdims=True), jnp.max(f, axis=1, keepdims=True))
        w = jnp.where(live, jnp.exp(s - m), 0.0)
        wf = jnp.where(fresh_live, jnp.exp(f - m), 0.0)
        total = jnp.sum(w, axis=1, keepdims=True) + jnp.sum(wf, axis=1, keepdims=True)
        wide = jnp.concatenate(
            [jnp.where(conv == b, w, 0.0).astype(bf16) for b in range(BATCH)], axis=1
        )
        o = mm(wide, values) + mm(wf.astype(bf16), vn_of(k))
        some = total > 0.0
        safe = jnp.where(some, total, 1.0)
        o = o * (1.0 / safe)
        lse = jnp.where(some, m + jnp.log(safe), NEGATIVE)
        hi = lse.astype(bf16).astype(f32)
        rest = lse - hi
        mid = rest.astype(bf16).astype(f32)
        low = rest - mid
        e = jnp.where(
            lane == width, hi, jnp.where(lane == width + 1, mid, jnp.where(lane == width + 2, low, 0.0))
        )
        for g in range(group):
            o_ref[k * group + g] = o[ROWS * g : ROWS * g + ROWS]
            e_ref[k * group + g] = e[ROWS * g : ROWS * g + ROWS]


def merged(x_ref, dev, width, groups):
    high = ROWS // groups
    span = 128 // groups
    n0 = jnp.minimum(width, 128 - (width * dev) % 128)
    a = iota((128, 128), 0)
    c = iota((128, 128), 1)
    start = jnp.where((c & (span - 1)) < n0, width, width + 3)
    delta = (a & (span - 1)) - start
    pick = ((a // span) == (c // span)) & (delta >= 0) & (delta < 3)
    pick = jnp.where(pick, 1.0, 0.0).astype(bf16)
    x = x_ref[...].astype(f32)
    lse = mm(x.reshape(DEV * high, 128).astype(bf16), pick).reshape(DEV, high, 128)
    peak = jnp.max(lse, axis=0)
    w = jnp.exp(lse - peak[None])
    return jnp.sum(w * x, axis=0) / jnp.sum(w, axis=0)


def k_qkv(dev_ref, x_ref, g_ref, w_ref, out_ref):
    scaled = (x_ref[...].astype(f32) * g_ref[...]).astype(bf16)[:, 0:FT]
    for h in range(HQ + 2 * HK):
        y = mm(scaled, w_ref[:, 128 * h : 128 * h + 128])
        for s in range(STEPS):
            j, i = divmod(4 * h + s, 3)
            out_ref[j, 8 * i : 8 * i + 8, :] = y[8 * s : 8 * s + 8].astype(bf16)
    for j in range(48, DEV):
        out_ref[j] = jnp.zeros((24, 128), bf16)


def k_rotate(dev_ref, x_ref, c_ref, s_ref, r_ref, out_ref):
    y = jnp.sum(x_ref[...].astype(f32), axis=0)
    parts = []
    for i in range(3):
        u = 3 * dev_ref[0] + i
        step = u & 3
        plain = u >= 4 * (HQ + HK)
        v = y[8 * i : 8 * i + 8]
        c = jnp.where(plain, jnp.ones((8, 128), f32), c_ref[step])
        s = jnp.where(plain, jnp.zeros((8, 128), f32), s_ref[step])
        parts.append((v * c + roll(v, 64) * s) * r_ref[step])
    z = jnp.concatenate(parts, axis=0).astype(bf16)
    out_ref[...] = jnp.broadcast_to(z[None], (DEV, 24, 128))


def k_text(dev_ref, q_ref, keys_ref, values_ref, limit_ref, out_ref, o_ref, e_ref):
    g = HQ // HK
    attend(
        lambda k: q_ref[ROWS * g * k : ROWS * g * (k + 1), :],
        lambda k: q_ref[ROWS * (HQ + k) : ROWS * (HQ + k + 1), :],
        lambda k: q_ref[ROWS * (HQ + HK + k) : ROWS * (HQ + HK + k + 1), :],
        keys_ref,
        values_ref,
        limit_ref[...],
        dev_ref[0],
        g,
        o_ref,
        e_ref,
        FT,
    )
    pack(out_ref, lambda h: o_ref[h], lambda h: e_ref[h], FT, 2)


def k_out(dev_ref, x_ref, w_ref, out_ref):
    att = unpack(merged(x_ref, dev_ref[0], FT, 2), 2).astype(bf16)[:, 0:FT]
    y = mm(att, w_ref[...])
    pack(out_ref, lambda h: y[:, 128 * h : 128 * h + 128], None, FT, 2)


def k_bridge(dev_ref, x_ref, in_ref, proj_ref, ids_ref, table_ref, hid_ref, out_ref):
    mine = in_ref[...].astype(f32)
    mine = mine[0:16] + roll(mine[16:32], 64)
    hid = (jnp.sum(x_ref[...].astype(f32), axis=0) + mine).astype(bf16)
    hid_ref[...] = hid
    rows = unpack(hid.astype(f32), 2).astype(bf16)[:, 0:FT]
    table = table_ref.shape[0]
    picked = ids_ref[...] - dev_ref[0] * table == iota((ROWS, table), 1)
    picked = jnp.where(picked, 1.0, 0.0).astype(bf16)
    y = mm(rows, proj_ref[...]) + mm(picked, table_ref[...])
    for s in range(STEPS):
        for n in range(TD // 128):
            out_ref[s * 7 + n] = y[8 * s : 8 * s + 8, 128 * n : 128 * n + 128].astype(bf16)
    for j in range(28, DEV):
        out_ref[j] = jnp.zeros((8, 128), bf16)


def k_spread(dev_ref, x_ref, hid_ref, out_ref):
    y = jnp.sum(x_ref[...].astype(f32), axis=0).astype(bf16)
    out_ref[:, 0:16, :] = jnp.broadcast_to(hid_ref[...][None], (DEV, 16, 128))
    out_ref[:, 16:24, :] = jnp.broadcast_to(y[None], (DEV, 8, 128))


def talker_rows(x_ref):
    return jnp.concatenate(
        [
            jnp.concatenate([x_ref[7 * s + n, 16:24, :].astype(f32) for n in range(7)], axis=1)
            for s in range(STEPS)
        ],
        axis=0,
    )


def k_audio(
    dev_ref, x_ref, gain_ref, w_ref, c_ref, s_ref, keys_ref, values_ref, limit_ref,
    out_ref, hidden_ref, q_ref, o_ref, e_ref,
):
    t = talker_rows(x_ref)
    factor = lax.rsqrt(jnp.sum(t * t, axis=1, keepdims=True) / TD + EPSILON)
    normed = (t * factor * gain_ref[...]).astype(bf16)
    c = c_ref[...].reshape(ROWS, 128)
    s = s_ref[...].reshape(ROWS, 128)
    y = mm(normed, w_ref[...])
    for h in range(AHQ + 2 * AHK):
        v = y[:, 128 * h : 128 * h + 128]
        if h < AHQ + AHK:
            v = v * c + roll(v, 64) * s
        q_ref[ROWS * h : ROWS * h + ROWS, :] = v.astype(bf16)
    g = AHQ // AHK
    attend(
        lambda k: q_ref[ROWS * g * k : ROWS * g * (k + 1), :],
        lambda k: q_ref[ROWS * (AHQ + k) : ROWS * (AHQ + k + 1), :],
        lambda k: q_ref[ROWS * (AHQ + AHK + k) : ROWS * (AHQ + AHK + k + 1), :],
        keys_ref,
        values_ref,
        limit_ref[...],
        dev_ref[0],
        g,
        o_ref,
        e_ref,
        FA,
    )
    pack(out_ref, lambda h: o_ref[h], lambda h: e_ref[h], FA, 4)
    lane = iota((16, 128), 1)
    for h in range(HQ):
        left = jnp.zeros((16, 128), f32)
        right = jnp.zeros((16, 128), f32)
        for j in range(128 * h // FT, (128 * h + 127) // FT + 1):
            at = FT * j - 128 * h
            tile = x_ref[j, 0:16, :].astype(f32)
            inside = (lane >= at) & (lane < at + FT)
            left = jnp.where(inside, roll(tile, at), left)
            right = jnp.where(inside, roll(tile, at - 64), right)
        hidden_ref[0:16, 128 * h : 128 * h + 128] = left.astype(bf16)
        hidden_ref[16:32, 128 * h : 128 * h + 128] = right.astype(bf16)


def k_heard(dev_ref, x_ref, t_ref, w_ref, out_ref):
    heard = unpack(merged(x_ref, dev_ref[0], FA, 4), 4).astype(bf16)[:, 0:FA]
    y = mm(heard, w_ref[...])
    y = y + jnp.where(dev_ref[0] == 0, talker_rows(t_ref), 0.0)
    pack(out_ref, lambda h: y[:, 128 * h : 128 * h + 128], None, CT, 4)


def k_last(dev_ref, x_ref, out_ref):
    y = jnp.sum(x_ref[...].astype(f32), axis=0)
    for s in range(STEPS):
        out_ref[s] = roll(y, -32 * s)[:, 0:CT].astype(bf16)


def swap(x):
    return lax.all_to_all(x, SEQ, 0, 0, tiled=True)


def tables(positions):
    half = HD // 2
    freqs = jnp.exp(jnp.arange(half).astype(f32) * (-2.0 * jnp.log(f32(THETA)) / HD))
    angles = positions.T.astype(f32)[:, :, None] * freqs[None, None, :]
    cosine = jnp.cos(angles)
    sine = jnp.sin(angles)
    return (
        jnp.concatenate([cosine, cosine], axis=-1),
        jnp.concatenate([-sine, sine], axis=-1),
    )


def body(
    thinker_input,
    thinker_gain,
    thinker_qkv,
    thinker_out,
    talker_proj,
    code_table,
    talker_gain,
    talker_qkv,
    talker_out,
    text_keys,
    text_values,
    audio_keys,
    audio_values,
    text_len,
    audio_len,
    text_pos,
    audio_pos,
    code_ids,
):
    index = lax.axis_index(SEQ)
    dev = index.reshape(1).astype(jnp.int32)
    shape = jax.ShapeDtypeStruct
    count = text_keys.shape[1]
    x = thinker_input.reshape(ROWS, D)
    mine = jnp.pad(lax.dynamic_slice_in_dim(x, index * FT, FT, 1), ((0, 0), (0, 128 - FT)))
    gain = jnp.pad(lax.dynamic_slice_in_dim(thinker_gain, index * FT, FT, 0), (0, 128 - FT))
    partial_qkv = call(k_qkv, shape((DEV, 24, 128), bf16), name="k_qkv", count=3)(
        dev, mine, gain.reshape(1, 128), thinker_qkv
    )
    wide = thinker_input.astype(f32)
    factor = lax.rsqrt(jnp.sum(wide * wide, axis=-1, keepdims=True) / D + EPSILON)
    factor = jnp.broadcast_to(factor, (STEPS, BATCH, 128))
    cosine, sine = tables(text_pos)
    audio_cosine, audio_sine = tables(audio_pos)
    text_limit = jnp.broadcast_to((text_len - index * count)[:, None], (BATCH, 128))
    audio_limit = jnp.broadcast_to((audio_len - index * count)[:, None], (BATCH, 128))
    ids = code_ids.T.reshape(ROWS, 1)
    out_rows = lax.dynamic_slice_in_dim(talker_out, index * FA, FA, 0)

    q = call(k_rotate, shape((DEV, 24, 128), bf16), name="k_rotate", count=4)(
        dev, swap(partial_qkv), cosine, sine, factor
    )
    q = swap(q).reshape(DEV * 24, 128)
    parts = call(
        k_text,
        shape((DEV, 16, 128), bf16),
        [VM((HQ, ROWS, 128), f32), VM((HQ, ROWS, 128), f32)],
        name="k_text",
        count=4,
    )(dev, q, text_keys, text_values, text_limit)
    parts = call(k_out, shape((DEV, 16, 128), bf16), name="k_out", count=2)(
        dev, swap(parts), thinker_out
    )
    hid, pieces = call(
        k_bridge, (shape((16, 128), bf16), shape((DEV, 8, 128), bf16)), name="k_bridge", count=5
    )(dev, swap(parts), mine, talker_proj, ids, code_table)
    both = call(k_spread, shape((DEV, 24, 128), bf16), name="k_spread", count=2)(
        dev, swap(pieces), hid
    )
    both = swap(both)
    parts, hidden = call(
        k_audio,
        (shape((DEV, 8, 128), bf16), shape((ROWS, D), bf16)),
        [
            VM(((AHQ + 2 * AHK) * ROWS, 128), bf16),
            VM((AHQ, ROWS, 128), f32),
            VM((AHQ, ROWS, 128), f32),
        ],
        name="k_audio",
        count=8,
    )(
        dev, both, talker_gain.reshape(1, TD), talker_qkv, audio_cosine, audio_sine,
        audio_keys, audio_values, audio_limit,
    )
    parts = call(k_heard, shape((DEV, 8, 128), bf16), name="k_heard", count=3)(
        dev, swap(parts), both, out_rows
    )
    talker = call(k_last, shape((STEPS, BATCH, CT), bf16), name="k_last", count=1)(
        dev, swap(parts)
    )
    return hidden.reshape(STEPS, BATCH, D), talker


def solution(mesh):
    placed = (
        P(None, "grp", None),
        P(),
        P(SEQ, None),
        P(SEQ, None),
        P(SEQ, None),
        P(SEQ, None),
        P(),
        P(),
        P(),
        P("grp", SEQ, None),
        P("grp", SEQ, None),
        P("grp", SEQ, None),
        P("grp", SEQ, None),
        P("grp"),
        P("grp"),
        P("grp", None),
        P("grp", None),
        P("grp", None),
    )
    return jax.shard_map(
        body,
        mesh=mesh,
        in_specs=placed,
        out_specs=(P(None, "grp", None), P(None, "grp", SEQ)),
        check_vma=False,
    )
```

time: 957 us -> 192 us (0.20); the launches traced: 944 us -> 191 us
  waiting for transfers between devices: 343 us -> 63.8 us
  blocking collectives: 317 us -> 51.6 us
  matrix products: 79.2 us -> 0 us
  local copies, waits for them, and re-layouts: 80.9 us -> 8.38 us
  other arithmetic: 71.9 us -> 4.06 us
  Pallas kernels: 0 us -> 29.4 us
  between operations: 17.4 us -> 0.76 us
    all_gather x24 -> x0, blocking collectives: 317 us -> none  [all_in_one(): both, at, found = (lax.all_gather(jnp.concatenate(lines), axis), 0, {})]
    psum x3 -> x0, waiting for transfers between devices: 157 us -> none  [by_axis(): return functools.reduce(lax.psum, axes, shard)]
    dot_general x56 -> x0, matrix products: 79.2 us -> none  [the longest x8 15.9 us: attend(): jnp.einsum('bkgt,btkd->bkgd', weight_cached.astype(jnp.bfloat16), value_f...]
    all_to_all x4 -> x5, waiting for transfers between devices: 129 us -> 63.8 us  [swap(): return lax.all_to_all(x, SEQ, 0, 0, tiled=True)]
    all_gather x4 -> x0, waiting for transfers between devices: 56.5 us -> none  [over_pieces(): return lax.all_gather(shard, axis).sum(0)]
    all_to_all x0 -> x3, blocking collectives: none -> 51.6 us  [swap(): return lax.all_to_all(x, SEQ, 0, 0, tiled=True)]
    convert_element_type x80 -> x0, local copies, waits for them, and re-layouts: 34.8 us -> none  [the longest x48 26.5 us: joined_all(): part[k].astype(own.dtype)]
    reduce_sum x23 -> x1, other arithmetic: 31.5 us -> 1.08 us  [body(): jnp.sum(wide * wide, axis=-1, keepdims=True) / D + EPSILON]
  transfers between devices with their start and end apart: 11 -> 5, of which waited for: 7 -> 5; matrix products, arithmetic and copies ran while one was open for 11% -> 3% of each run, Pallas kernels for 0% -> 0%
where the time goes in v1:
time: 192 us; the launch traced here: 191 us
  waiting for transfers between devices  63.8 us (33%)
  blocking collectives  51.6 us (27%)
  starting transfers between devices  33.2 us (17%)
  Pallas kernels  29.4 us (15%)
  local copies, waits for them, and re-layouts  8.38 us (4%)
  other arithmetic  4.06 us (2%)
    all_to_all x5, waiting for transfers between devices, swap(): return lax.all_to_all(x, SEQ, 0, 0, tiled=True)  63.8 us
    all_to_all x3, blocking collectives, swap(): return lax.all_to_all(x, SEQ, 0, 0, tiled=True)  51.6 us
    all_to_all x5, starting transfers between devices, swap(): return lax.all_to_all(x, SEQ, 0, 0, tiled=True)  33.2 us
    pallas_call x1, Pallas kernels, body(): call(k_text, shape((DEV, 16, 128), bf16), [VM((HQ, ROWS, 128), f32), VM((...  7.24 us
    pallas_call x1, Pallas kernels, body(): call(k_audio, (shape((DEV, 8, 128), bf16), shape((ROWS, D), bf16)), [VM((...  6.95 us
  transfers between devices with their start and end apart: 5, of which 5 were waited for; matrix products, arithmetic and copies ran while one was open for 3% of the time, Pallas kernels for 0%

profile of v1, /device:TPU:1, one launch (start us, length us, event | category | flops | bytes accessed | tf_op | source)
XLA Modules:
  0.0 191.2 jit_solution(2446139806862291208)
XLA Ops:
  0.6 0.0 copy-start
  0.6 0.0 copy-start.8
  0.7 1.0 constant_dynamic-slice_fusion.1
  1.6 0.8 dynamic_slice.10
  2.4 0.5 pad_bitcast_fusion.g_ref
  2.9 0.6 pad.8.x_ref.in_ref
  3.5 2.1 %k_qkv.1 = bf16[64,24,128]{2,1,0:T(8,128)(2,1)} custom-call(s32[1]{0:T(128)} %bitcast.dev_ref, bf16[32,128]{1,0:T(8,128)(2,1)} %pad.8.x_ref.in_ref, f32[1,128]{1,0:T(1,128)} %pad_bitcast_fusion.g_ref, bf16[56,4608]{1,0:T(8,128)(2,1)} %w_ref.3), custom_call_target="tpu_custom_call" | custom-call | tf_op jit(solution)/shard_map/k_qkv/pallas_call | solution.py:336
  5.6 13.0 %all-to-all-start = ((bf16[64,24,128]{2,1,0:T(8,128)(2,1)}), bf16[64,24,128]{2,1,0:T(8,128)(2,1)S(1)}, u32[]{:S(2)}, u32[]{:S(2)}) async-start(bf16[64,24,128]{2,1,0:T(8,128)(2,1)} %k_qkv.1), calls=%async_computation | async-start | bytes 786432 | tf_op jit(solution)/shard_map/all_to_all | solution.py:294
  18.6 0.7 convert_bitcast_fusion
  19.3 0.7 convert_bitcast_fusion.1
  20.0 0.2 fusion.1
  20.2 0.7 pad_maximum_fusion
  20.9 1.1 multiply_reduce_fusion
  21.9 11.8 %all-to-all-done.x_ref = bf16[64,24,128]{2,1,0:T(8,128)(2,1)S(1)} async-done(((bf16[64,24,128]{2,1,0:T(8,128)(2,1)}), bf16[64,24,128]{2,1,0:T(8,128)(2,1)S(1)}, u32[]{:S(2)}, u32[]{:S(2)}) %all-to-all-start) | async-done | bytes 393248 | tf_op jit(solution)/shard_map/all_to_all | solution.py:294
  33.7 0.0 copy-start.2
  33.7 0.8 broadcast_in_dim.6.r_ref
  34.5 0.0 copy-done.2
  34.5 1.9 %k_rotate.1 = bf16[64,24,128]{2,1,0:T(8,128)(2,1)} custom-call(s32[1]{0:T(128)} %bitcast.dev_ref, bf16[64,24,128]{2,1,0:T(8,128)(2,1)} %copy-done.2, f32[4,8,128]{2,1,0:T(8,128)} %get-tuple-element.19.c_ref, f32[4,8,128]{2,1,0:T(8,128)} %get-tuple-element.20.s_ref, f32[4,8,128]{2,1,0:T(8,128)} %broadcast_in_dim.6.r_ref), custom_call_target="tpu_custom_call" | custom-call | tf_op jit(solution)/shard_map/k_rotate/pallas_call | solution.py:349
  36.5 0.0 copy-start.7
  36.5 5.6 %all-to-all-start.1 = ((bf16[64,24,128]{2,1,0:T(8,128)(2,1)}), bf16[64,24,128]{2,1,0:T(8,128)(2,1)S(1)}, u32[]{:S(2)}, u32[]{:S(2)}) async-start(bf16[64,24,128]{2,1,0:T(8,128)(2,1)} %k_rotate.1), calls=%async_computation.1 | async-start | bytes 786432 | tf_op jit(solution)/shard_map/all_to_all | solution.py:294
  42.1 0.0 copy-done.8
  42.1 15.1 %all-to-all-done.1 = bf16[64,24,128]{2,1,0:T(8,128)(2,1)S(1)} async-done(((bf16[64,24,128]{2,1,0:T(8,128)(2,1)}), bf16[64,24,128]{2,1,0:T(8,128)(2,1)S(1)}, u32[]{:S(2)}, u32[]{:S(2)}) %all-to-all-start.1) | async-done | bytes 393248 | tf_op jit(solution)/shard_map/all_to_all | solution.py:294
  57.2 0.0 copy-start.3
  57.2 0.7 broadcast_in_dim.7.limit_ref
  57.9 0.0 copy-done.3
  58.0 7.2 %k_text.1 = bf16[64,16,128]{2,1,0:T(8,128)(2,1)} custom-call(s32[1]{0:T(128)} %bitcast.dev_ref, bf16[1536,128]{1,0:T(8,128)(2,1)} %bitcast.11, bf16[8,128,512]{2,1,0:T(8,128)(2,1)} %keys_ref.2, bf16[8,128,512]{2,1,0:T(8,128)(2,1)} %values_ref.2, s32[8,128]{1,0:T(8,128)} %broadcast_in_dim.7.limit_ref), custom_call_target="tpu_custom_call" | custom-call | tf_op jit(solution)/shard_map/k_text/pallas_call | solution.py:353
  65.2 0.0 copy-start.6
  65.2 0.0 copy-start.9
  65.2 18.8 %all_to_all.40.x_ref = bf16[64,16,128]{2,1,0:T(8,128)(2,1)} all-to-all(bf16[64,16,128]{2,1,0:T(8,128)(2,1)} %k_text.1), channel_id=1, replica_groups=mesh['grp'=4,'seq'=64] {'seq'}, dimensions={0} | all-to-all | bytes 524288 | tf_op jit(solution)/shard_map/all_to_all | solution.py:294
  84.0 3.0 %k_out.1 = bf16[64,16,128]{2,1,0:T(8,128)(2,1)} custom-call(s32[1]{0:T(128)} %bitcast.dev_ref, bf16[64,16,128]{2,1,0:T(8,128)(2,1)} %all_to_all.40.x_ref, bf16[56,3584]{1,0:T(8,128)(2,1)} %w_ref.4), custom_call_target="tpu_custom_call" | custom-call | tf_op jit(solution)/shard_map/k_out/pallas_call | solution.py:360
  87.0 4.8 %all-to-all-start.3 = ((bf16[64,16,128]{2,1,0:T(8,128)(2,1)}), bf16[64,16,128]{2,1,0:T(8,128)(2,1)S(1)}, u32[]{:S(2)}, u32[]{:S(2)}) async-start(bf16[64,16,128]{2,1,0:T(8,128)(2,1)} %k_out.1), calls=%async_computation.3 | async-start | bytes 524288 | tf_op jit(solution)/shard_map/all_to_all | solution.py:294
  91.8 0.0 copy-done.7
  91.8 0.7 reshape.50.ids_ref
  92.4 12.4 %all-to-all-done.3.x_ref = bf16[64,16,128]{2,1,0:T(8,128)(2,1)S(1)} async-done(((bf16[64,16,128]{2,1,0:T(8,128)(2,1)}), bf16[64,16,128]{2,1,0:T(8,128)(2,1)S(1)}, u32[]{:S(2)}, u32[]{:S(2)}) %all-to-all-start.3) | async-done | bytes 262176 | tf_op jit(solution)/shard_map/all_to_all | solution.py:294
  104.8 0.0 copy-start.4
  104.8 0.7 copy-done.4
  105.5 2.1 %k_bridge.1 = (bf16[16,128]{1,0:T(8,128)(2,1)}, bf16[64,8,128]{2,1,0:T(8,128)(2,1)}) custom-call(s32[1]{0:T(128)} %bitcast.dev_ref, bf16[64,16,128]{2,1,0:T(8,128)(2,1)} %copy-done.4, bf16[32,128]{1,0:T(8,128)(2,1)} %pad.8.x_ref.in_ref, bf16[56,896]{1,0:T(8,128)(2,1)} %proj_ref.1, s32[32,1]{1,0:T(8,128)} %reshape.50.ids_ref, bf16[132,896]{1,0:T(8,128)(2,1)} %table_ref.1), custom_call_target="tpu_custom_call" | custom-call | tf_op jit(solution)/shard_map/k_bridge/pallas_call | solution.py:363
  107.6 16.4 %all_to_all.41.x_ref = bf16[64,8,128]{2,1,0:T(8,128)(2,1)} all-to-all(bf16[64,8,128]{2,1,0:T(8,128)(2,1)} %get-tuple-element.6), channel_id=1, replica_groups=mesh['grp'=4,'seq'=64] {'seq'}, dimensions={0} | all-to-all | bytes 262144 | tf_op jit(solution)/shard_map/all_to_all | solution.py:294
  124.0 1.8 k_spread.1
  125.7 4.5 %all-to-all-start.5 = ((bf16[64,24,128]{2,1,0:T(8,128)(2,1)}), bf16[64,24,128]{2,1,0:T(8,128)(2,1)S(1)}, u32[]{:S(2)}, u32[]{:S(2)}) async-start(bf16[64,24,128]{2,1,0:T(8,128)(2,1)} %k_spread.1), calls=%async_computation.5 | async-start | bytes 786432 | tf_op jit(solution)/shard_map/all_to_all | solution.py:294
  130.2 0.0 copy-done.6
  130.2 0.6 reshape.48.gain_ref
  130.8 0.7 pad_maximum_fusion.2
  131.5 0.0 copy-done.9
  131.5 14.0 %all-to-all-done.5.x_ref.t_ref = bf16[64,24,128]{2,1,0:T(8,128)(2,1)S(1)} async-done(((bf16[64,24,128]{2,1,0:T(8,128)(2,1)}), bf16[64,24,128]{2,1,0:T(8,128)(2,1)S(1)}, u32[]{:S(2)}, u32[]{:S(2)}) %all-to-all-start.5) | async-done | bytes 393248 | tf_op jit(solution)/shard_map/all_to_all | solution.py:294
  145.5 0.0 copy-start.1
  145.5 0.7 broadcast_in_dim.8.limit_ref
  146.3 0.0 copy-done.1
  146.3 6.9 %k_audio.1 = (bf16[64,8,128]{2,1,0:T(8,128)(2,1)}, bf16[32,3584]{1,0:T(8,128)(2,1)}) custom-call(s32[1]{0:T(128)} %bitcast.dev_ref, bf16[64,24,128]{2,1,0:T(8,128)(2,1)} %copy-done.1, f32[1,896]{1,0:T(1,128)} %reshape.48.gain_ref, bf16[896,2560]{1,0:T(8,128)(2,1)} %w_ref.5, f32[4,8,128]{2,1,0:T(8,128)} %get-tuple-element.21.c_ref, ...), custom_call_target="tpu_custom_call" | custom-call | tf_op jit(solution)/shard_map/k_audio/pallas_call | solution.py:370
  153.2 5.4 %all-to-all-start.6 = ((bf16[64,8,128]{2,1,0:T(8,128)(2,1)}), bf16[64,8,128]{2,1,0:T(8,128)(2,1)S(1)}, u32[]{:S(2)}, u32[]{:S(2)}) async-start(bf16[64,8,128]{2,1,0:T(8,128)(2,1)} %get-tuple-element.9), calls=%async_computation.6 | async-start | bytes 262144 | tf_op jit(solution)/shard_map/all_to_all | solution.py:294
  158.6 0.0 copy-done
  158.6 0.6 constant_dynamic-slice_fusion.w_ref
  159.3 10.5 %all-to-all-done.6.x_ref = bf16[64,8,128]{2,1,0:T(8,128)(2,1)S(1)} async-done(((bf16[64,8,128]{2,1,0:T(8,128)(2,1)}), bf16[64,8,128]{2,1,0:T(8,128)(2,1)S(1)}, u32[]{:S(2)}, u32[]{:S(2)}) %all-to-all-start.6) | async-done | bytes 131104 | tf_op jit(solution)/shard_map/all_to_all | solution.py:294
  169.7 0.0 copy-start.5
  169.7 0.7 copy-done.5
  170.4 2.7 %k_heard.1 = bf16[64,8,128]{2,1,0:T(8,128)(2,1)} custom-call(s32[1]{0:T(128)} %bitcast.dev_ref, bf16[64,8,128]{2,1,0:T(8,128)(2,1)} %copy-done.5, bf16[64,24,128]{2,1,0:T(8,128)(2,1)} %copy-done.1, bf16[24,896]{1,0:T(8,128)(2,1)} %constant_dynamic-slice_fusion.w_ref), custom_call_target="tpu_custom_call" | custom-call | tf_op jit(solution)/shard_map/k_heard/pallas_call | solution.py:384
  173.1 16.5 %all_to_all.42.x_ref = bf16[64,8,128]{2,1,0:T(8,128)(2,1)} all-to-all(bf16[64,8,128]{2,1,0:T(8,128)(2,1)} %k_heard.1), channel_id=1, replica_groups=mesh['grp'=4,'seq'=64] {'seq'}, dimensions={0} | all-to-all | bytes 262144 | tf_op jit(solution)/shard_map/all_to_all | solution.py:294
  189.6 1.6 k_last.1
  (4 shorter events, 0.0 us)
Async XLA Ops:
  0.6 158.0 %copy-start = (bf16[1536,896]{1,0:T(8,128)(2,1)S(1)}, bf16[1536,896]{1,0:T(8,128)(2,1)}, u32[]{:S(2)}) copy-start(bf16[1536,896]{1,0:T(8,128)(2,1)} %param.26) | copy-start | bytes 8257540
  0.6 41.4 %copy-start.8 = (s32[8]{0:T(128)S(1)}, s32[8]{0:T(128)}, u32[]{:S(2)}) copy-start(s32[8]{0:T(128)} %param.31) | copy-start | bytes 100
  5.6 28.1 %all-to-all-start = ((bf16[64,24,128]{2,1,0:T(8,128)(2,1)}), bf16[64,24,128]{2,1,0:T(8,128)(2,1)S(1)}, u32[]{:S(2)}, u32[]{:S(2)}) async-start(bf16[64,24,128]{2,1,0:T(8,128)(2,1)} %k_qkv.1), calls=%async_computation | async-start | bytes 786432 | tf_op jit(solution)/shard_map/all_to_all | solution.py:294
  33.7 0.8 copy-start.2
  36.5 55.3 %copy-start.7 = (s32[8,4]{0,1:T(4,128)S(1)}, s32[8,4]{0,1:T(4,128)}, u32[]{:S(2)}) copy-start(s32[8,4]{0,1:T(4,128)} %param.35) | copy-start | bytes 388
  36.5 20.8 %all-to-all-start.1 = ((bf16[64,24,128]{2,1,0:T(8,128)(2,1)}), bf16[64,24,128]{2,1,0:T(8,128)(2,1)S(1)}, u32[]{:S(2)}, u32[]{:S(2)}) async-start(bf16[64,24,128]{2,1,0:T(8,128)(2,1)} %k_rotate.1), calls=%async_computation.1 | async-start | bytes 786432 | tf_op jit(solution)/shard_map/all_to_all | solution.py:294
  57.2 0.8 copy-start.3
  65.2 65.0 %copy-start.6 = (f32[896]{0:T(1024)S(1)}, f32[896]{0:T(1024)}, u32[]{:S(2)}) copy-start(f32[896]{0:T(1024)} %param.24) | copy-start | bytes 10756
  65.2 66.3 %copy-start.9 = (s32[8]{0:T(128)S(1)}, s32[8]{0:T(128)}, u32[]{:S(2)}) copy-start(s32[8]{0:T(128)} %param.32) | copy-start | bytes 100
  87.0 17.9 %all-to-all-start.3 = ((bf16[64,16,128]{2,1,0:T(8,128)(2,1)}), bf16[64,16,128]{2,1,0:T(8,128)(2,1)S(1)}, u32[]{:S(2)}, u32[]{:S(2)}) async-start(bf16[64,16,128]{2,1,0:T(8,128)(2,1)} %k_out.1), calls=%async_computation.3 | async-start | bytes 524288 | tf_op jit(solution)/shard_map/all_to_all | solution.py:294
  104.8 0.7 copy-start.4
  125.7 19.8 %all-to-all-start.5 = ((bf16[64,24,128]{2,1,0:T(8,128)(2,1)}), bf16[64,24,128]{2,1,0:T(8,128)(2,1)S(1)}, u32[]{:S(2)}, u32[]{:S(2)}) async-start(bf16[64,24,128]{2,1,0:T(8,128)(2,1)} %k_spread.1), calls=%async_computation.5 | async-start | bytes 786432 | tf_op jit(solution)/shard_map/all_to_all | solution.py:294
  145.5 0.8 copy-start.1
  153.2 16.5 %all-to-all-start.6 = ((bf16[64,8,128]{2,1,0:T(8,128)(2,1)}), bf16[64,8,128]{2,1,0:T(8,128)(2,1)S(1)}, u32[]{:S(2)}, u32[]{:S(2)}) async-start(bf16[64,8,128]{2,1,0:T(8,128)(2,1)} %get-tuple-element.9), calls=%async_computation.6 | async-start | bytes 262144 | tf_op jit(solution)/shard_map/all_to_all | solution.py:294
  169.7 0.7 copy-start.5
